TPU v7x, 128 devices: a whole 4x4x4 slice. The times are simulated.
128 devices in a mesh: dev: 128 (over z, x, y, core).
Axes of the slice: x: 4, y: 4, z: 4, core: 2. Of those that a mesh axis runs over, the one named last changes fastest.
Arguments:
- occurrence: bfloat16 [8192, 128, 128], P('dev'), may hold values from -0.5 to 0.5
- block_owner: int32 [8192, 1], P('dev'), may hold values from 0 to 127; in each aligned block of 64 rows (0 to 63, 64 to 127, ...) no two rows name the same one
- read_block: int32 [8192], P('dev'), may hold values from 0 to 15
- slot_order: int32 [128, 128], P('dev'), may hold values from 0 to 127, each once within a row
Outputs:
- margin: float32 [262144, 512], P('dev')
Inputs may be any that keep to these rules, and one draw needn't show every extreme that they name: `block_owner`: among the blocks of one device no owner is named more than 1 times, a bound that some block reaches. `slot_order`: each row names every number of 0 to 127 once.
All inputs are finite; a program needn't handle non-finite values.
Results may differ from a plain program's by a relative error of at most 0.0026.
Values may be sent and summed in bfloat16 or wider, within the bound.
No kernel may reach another device: no remote copies, remote signals or barrier semaphores. Data moves between devices by JAX's collectives and lax.ppermute only.
A program may use at most 128 MiB of HBM per device.

v0:
```python
import jax
import jax.numpy as jnp
from jax import lax
from jax.sharding import PartitionSpec as P

CAP = 4
RB_DEV = 16


def shards(occurrence, block_owner, read_block, slot_order):
    devices = lax.axis_size("dev")
    blocks, rows, kmers = occurrence.shape
    per_pair = 2 * blocks // devices
    slot_total = devices * per_pair
    owners = block_owner[:, 0]
    positions = jnp.arange(blocks, dtype=jnp.int32)
    earlier = positions[None, :] < positions[:, None]
    same_owner = owners[:, None] == owners[None, :]
    earlier_count = jnp.sum((same_owner & earlier).astype(jnp.int32), axis=1)
    send_slot = owners * per_pair + earlier_count
    onehot = (send_slot[:, None] == jnp.arange(slot_total, dtype=jnp.int32)[None, :]).astype(
        jnp.bfloat16
    )
    outgoing = jnp.einsum(
        "bs,bik->sik", onehot, occurrence, preferred_element_type=jnp.float32
    ).astype(jnp.bfloat16)
    received = lax.all_to_all(outgoing, "dev", split_axis=0, concat_axis=0, tiled=True)
    order_row = slot_order[0]
    place_of = (
        jnp.zeros((slot_total,), jnp.int32)
        .at[order_row]
        .set(jnp.arange(slot_total, dtype=jnp.int32))
    )
    groups = received[order_row].reshape(slot_total // CAP, CAP, rows, kmers)
    read_onehot = (read_block[None, :] == jnp.arange(RB_DEV, dtype=jnp.int32)[:, None]).astype(
        jnp.bfloat16
    )
    tile_block = jnp.einsum("gpik,gjrk->gpijr", groups, groups, preferred_element_type=jnp.float32)
    tile_block = tile_block.astype(jnp.bfloat16).reshape(slot_total, rows, CAP * rows)
    tile_slot = tile_block[place_of]
    returned = lax.all_to_all(tile_slot, "dev", split_axis=0, concat_axis=0, tiled=True)
    placement = jnp.dot(read_onehot, onehot, preferred_element_type=jnp.float32).astype(
        jnp.bfloat16
    )
    summed = jnp.einsum("ns,sic->nic", placement, returned, preferred_element_type=jnp.float32)
    return summed.reshape(RB_DEV * rows, CAP * rows)


def solution(mesh):
    placed = (P("dev", None, None), P("dev", None), P("dev"), P("dev", None))
    return jax.shard_map(
        shards, mesh=mesh, in_specs=placed, out_specs=P("dev", None), check_vma=False
    )
```

profile of v0, /device:TPU:1, one launch (start us, length us, event | category | flops | bytes accessed | tf_op | source)
XLA Modules:
  0.0 344.2 jit_solution(17272551943386160158)
XLA Ops:
  0.0 0.0 copy-start
  0.0 1.0 convert_reduce_fusion
  1.0 0.7 fusion.13
  1.7 0.0 copy-done
  1.7 2.0 convolution_convert_fusion.1
  3.7 4.7 %copy.19 = bf16[128,128,128]{2,1,0:T(8,128)(2,1)} copy(bf16[128,128,128]{2,0,1:T(8,128)(2,1)S(1)} %convolution_convert_fusion.1) | data formatting | bytes 8388608 | tf_op jit(solution)/shard_map/convert_element_type | solution.py:26
  8.4 0.0 copy-start.3
  8.4 11.9 %all-to-all-start = ((bf16[128,128,128]{2,1,0:T(8,128)(2,1)}), bf16[128,128,128]{2,1,0:T(8,128)(2,1)}, u32[]{:S(2)}, u32[]{:S(2)}) async-start(bf16[128,128,128]{2,1,0:T(8,128)(2,1)} %copy.19), calls=%async_computation | async-start | bytes 8388608 | tf_op jit(solution)/shard_map/all_to_all | solution.py:27
  20.4 0.0 copy-done.3
  20.4 1.0 scatter_custom_fusion
  21.4 51.7 %all-to-all-done = bf16[128,128,128]{2,1,0:T(8,128)(2,1)} async-done(((bf16[128,128,128]{2,1,0:T(8,128)(2,1)}), bf16[128,128,128]{2,1,0:T(8,128)(2,1)}, u32[]{:S(2)}, u32[]{:S(2)}) %all-to-all-start) | async-done | bytes 4194336 | tf_op jit(solution)/shard_map/all_to_all | solution.py:27
  73.1 5.3 %gather_fusion = bf16[128,128,128]{2,1,0:T(8,128)(2,1)} fusion(bf16[128,128,128]{2,1,0:T(8,128)(2,1)} %all-to-all-done, s32[1024]{0:T(1024)S(1)} %pad_clamp_fusion.1), kind=kCustom, calls=%fused_computation | custom fusion | bytes 8389120 | tf_op jit(solution)/shard_map/gather | solution.py:34
  78.4 10.9 %convolution_convert_fusion = bf16[32,4,128,4,128]{2,4,3,1,0:T(8,128)(2,1)} fusion(bf16[32,4,128,128,1]{3,2,4,1,0:T(8,128)(2,1)} %bitcast.31, bf16[32,4,128,128,1]{3,2,1,4,0:T(8,128)(2,1)} %bitcast.32), kind=kOutput, calls=%fused_computation.5 | convolution fusion | flops 2155872256 | bytes 25165824 | tf_op jit(solution)/shard_map/gpik,gjrk->gpijr/dot_general | solution.py:38
  89.3 22.4 %copy.20 = bf16[128,128,512]{2,1,0:T(8,128)(2,1)} copy(bf16[128,128,512]{1,2,0:T(8,128)(2,1)} %bitcast.30) | data formatting | bytes 33554432 | tf_op jit(solution)/shard_map/reshape | solution.py:39
  111.7 14.1 %gather_fusion.1 = bf16[128,128,512]{2,1,0:T(8,128)(2,1)} fusion(bf16[128,128,512]{2,1,0:T(8,128)(2,1)} %copy.20, s32[1024]{0:T(1024)S(1)} %pad_clamp_fusion), kind=kCustom, calls=%fused_computation.1 | custom fusion | bytes 33554944 | tf_op jit(solution)/shard_map/gather | solution.py:40
  125.8 0.0 copy-start.2
  125.8 193.7 %all_to_all.10 = bf16[128,128,512]{2,1,0:T(8,128)(2,1)} all-to-all(bf16[128,128,512]{2,1,0:T(8,128)(2,1)} %gather_fusion.1), channel_id=1, replica_groups=mesh['dev'=128] {'dev'}, dimensions={0} | all-to-all | bytes 33554432 | tf_op jit(solution)/shard_map/all_to_all | solution.py:41
  319.5 0.0 copy-done.2
  319.5 0.0 copy-start.1
  319.5 18.1 %fusion = f32[16,128,512]{2,0,1:T(8,128)} fusion(bf16[128,128,512]{2,1,0:T(8,128)(2,1)} %all_to_all.10, s32[64]{0:T(128)S(1)} %fusion.13, s32[64]{0:T(128)S(1)} %copy-done.2), kind=kOutput, calls=%fused_computation.3 | convolution fusion | flops 268708864 | bytes 20972032 | tf_op jit(solution)/shard_map/ns,sic->nic/dot_general | solution.py:45
  337.6 6.6 %copy.22 = f32[16,128,512]{2,1,0:T(8,128)} copy(f32[16,128,512]{2,0,1:T(8,128)} %fusion) | data formatting | bytes 8388608 | tf_op jit(solution)/shard_map/ns,sic->nic/dot_general | solution.py:45
  344.2 0.0 copy-done.1
  (5 shorter events, 0.0 us)
Async XLA Ops:
  0.0 1.7 copy-start
  8.4 12.0 %copy-start.3 = (s32[1,128]{1,0:T(1,128)S(1)}, s32[1,128]{1,0:T(1,128)}, u32[]{:S(2)}) copy-start(s32[1,128]{1,0:T(1,128)} %param.7) | copy-start | bytes 1540
  8.4 64.7 %all-to-all-start = ((bf16[128,128,128]{2,1,0:T(8,128)(2,1)}), bf16[128,128,128]{2,1,0:T(8,128)(2,1)}, u32[]{:S(2)}, u32[]{:S(2)}) async-start(bf16[128,128,128]{2,1,0:T(8,128)(2,1)} %copy.19), calls=%async_computation | async-start | bytes 8388608 | tf_op jit(solution)/shard_map/all_to_all | solution.py:27
  125.8 193.7 %copy-start.2 = (s32[64]{0:T(128)S(1)}, s32[64]{0:T(128)}, u32[]{:S(2)}) copy-start(s32[64]{0:T(128)} %param.6) | copy-start | bytes 772
  319.5 24.8 %copy-start.1 = (bf16[64,128,128]{2,1,0:T(8,128)(2,1)S(1)}, bf16[64,128,128]{2,1,0:T(8,128)(2,1)}, u32[]{:S(2)}) copy-start(bf16[64,128,128]{2,1,0:T(8,128)(2,1)} %param.4) | copy-start | bytes 6291460
where the time goes:
time: 345 us; the launch traced here: 344 us
  blocking collectives  194 us (56%)
  local copies, waits for them, and re-layouts  54.1 us (16%)
  waiting for transfers between devices  51.7 us (15%)
  matrix products  31.1 us (9%)
  starting transfers between devices  11.9 us (3%)
    all_to_all x1, blocking collectives, shards(): lax.all_to_all(tile_slot, 'dev', split_axis=0, concat_axis=0, tiled=True)  194 us
    all_to_all x1, waiting for transfers between devices, shards(): lax.all_to_all(outgoing, 'dev', split_axis=0, concat_axis=0, tiled=True)  51.7 us
    reshape x1, local copies, waits for them, and re-layouts, shards(): tile_block.astype(jnp.bfloat16).reshape(slot_total, rows, CAP * rows)  22.4 us
    dot_general x1, matrix products, shards(): jnp.einsum('ns,sic->nic', placement, returned, preferred_element_type=jnp...  18.1 us
    gather x1, local copies, waits for them, and re-layouts, shards(): tile_slot = tile_block[place_of]  14.1 us
    all_to_all x1, starting transfers between devices, shards(): lax.all_to_all(outgoing, 'dev', split_axis=0, concat_axis=0, tiled=True)  11.9 us
    dot_general x1, matrix products, shards(): jnp.einsum('gpik,gjrk->gpijr', groups, groups, preferred_element_type=jnp...  10.9 us
  transfers between devices with their start and end apart: 1, of which 1 were waited for; matrix products, arithmetic and copies ran while one was open for 0% of the time, Pallas kernels for 0%

commit v1 on v0

v1 whole, which is shorter than its diff:
```python
import jax
import jax.numpy as jnp
from jax import lax
from jax.experimental import pallas as pl
from jax.experimental.pallas import tpu as pltpu
from jax.sharding import PartitionSpec as P

CAP = 4
RB_DEV = 16
LIST = 256
ROOMS = (128, 144)
CHUNK = 16


def lists_kernel(me_ref, read_ref, shared_ref, list_ref, plan_ref, most_ref, order_ref, owner_ref, rank_ref, value_ref):
    f32, bf16 = jnp.float32, jnp.bfloat16
    devices = shared_ref.shape[0]
    blocks = read_ref.shape[1]
    square = (devices, devices)
    most = (CAP - 1) * blocks

    def iota(shape, axis):
        return lax.broadcasted_iota(jnp.int32, shape, axis).astype(f32)

    order = shared_ref[:, :devices]
    order_ref[...] = order.astype(f32).T
    owner_ref[...] = shared_ref[:, devices : 2 * devices].astype(f32).T
    row, lane = iota(square, 0), iota(square, 1)

    def hold(n, held):
        return jnp.where(owner_ref[pl.ds(n, 1), :] == row, (n + 1).astype(f32), held)

    def stand(q, place):
        return jnp.where(order_ref[pl.ds(q, 1), :] == row, q.astype(f32), place)

    held = lax.fori_loop(0, blocks, hold, jnp.zeros(square, f32))
    place = lax.fori_loop(0, devices, stand, jnp.zeros(square, f32)).T.astype(jnp.int32)
    there = jnp.take_along_axis(held, order, axis=1)
    number = jnp.where(there > 0.0, order.astype(f32) * blocks + there, 0.0)
    values = [
        jnp.where(held > 0.0, jnp.take_along_axis(number, place ^ j, axis=1), 0.0)
        for j in range(1, CAP)
    ]
    needs = [(v > 0.0).astype(f32) for v in values]
    total = needs[0] + needs[1] + needs[2]
    below = (lane < row).astype(f32).astype(bf16)
    rank = jnp.dot(below, total.astype(bf16), preferred_element_type=f32)
    ranks = []
    for j in range(CAP - 1):
        ranks.append(jnp.where(needs[j] > 0.0, rank, -1.0))
        rank = rank + needs[j]
        rank_ref[j] = ranks[j]
        value_ref[j] = values[j] - 1.0
    count = jnp.max(rank[devices - 1 :, :])
    most_ref[0] = sum((count > room).astype(jnp.int32) for room in ROOMS)
    turn = iota((most, devices), 0)

    def fill(o, found):
        for j in range(CAP - 1):
            hit = rank_ref[j, pl.ds(o, 1), :] == turn
            found = jnp.where(hit, value_ref[j, pl.ds(o, 1), :], found)
        return found

    found = lax.fori_loop(0, devices, fill, jnp.zeros((most, devices), f32))
    list_ref[:, :devices] = found[:devices].T.astype(jnp.int32)
    rest = jnp.concatenate([found[devices:], jnp.zeros((LIST - most, devices), f32)], axis=0)
    list_ref[:, devices:] = rest.T.astype(jnp.int32)

    me = me_ref[0].astype(f32)

    def mine(array):
        return jnp.sum(jnp.where(lane == me, array, 0.0), axis=1, keepdims=True)

    reads = read_ref[...].astype(f32)
    row, column = iota((blocks, blocks), 0), iota((blocks, blocks), 1)
    read = jnp.sum(jnp.where(row == column, reads, 0.0), axis=1, keepdims=True)
    before = (read < reads) | ((read == reads) & (row < column))
    at = jnp.sum(before.astype(f32), axis=0, keepdims=True)
    own = mine(held)
    chosen = own == iota((devices, blocks), 1) + 1.0
    at = jnp.sum(jnp.where(chosen, at, 0.0), axis=1, keepdims=True)
    read = jnp.sum(jnp.where(chosen, reads, 0.0), axis=1, keepdims=True)
    turn = (at == lane) & (own > 0.0)
    stands = mine((place & (CAP - 1)).astype(f32))
    spots = [-1.0 - own] + [mine(r) for r in ranks]
    rows = []
    for j in range(CAP):
        spot = jnp.zeros_like(own)
        for p in range(CAP):
            spot = jnp.where(stands == float(p), spots[p ^ j], spot)
        rows.append(jnp.sum(jnp.where(turn, spot, 0.0), axis=0, keepdims=True))
    rows.append(jnp.sum(jnp.where(turn, own - 1.0, 0.0), axis=0, keepdims=True))
    by_read = jnp.sum(jnp.where(turn, read, 0.0), axis=0, keepdims=True)
    rows.append(jnp.where(iota((1, devices), 1) < blocks, by_read, float(RB_DEV)))
    rows += [jnp.zeros((1, devices), f32)] * 2
    plan_ref[...] = jnp.concatenate(rows, axis=0).astype(jnp.int32)


def lists(me, read, shared):
    devices = shared.shape[0]
    whole = pl.BlockSpec(memory_space=pltpu.VMEM)
    small = pl.BlockSpec(memory_space=pltpu.SMEM)
    return pl.pallas_call(
        lists_kernel,
        in_specs=[small, whole, whole],
        out_specs=(whole, whole, small),
        out_shape=(
            jax.ShapeDtypeStruct((devices, LIST), jnp.int32),
            jax.ShapeDtypeStruct((8, devices), jnp.int32),
            jax.ShapeDtypeStruct((1,), jnp.int32),
        ),
        scratch_shapes=[
            pltpu.VMEM((devices, devices), jnp.float32),
            pltpu.VMEM((devices, devices), jnp.float32),
            pltpu.VMEM((CAP - 1, devices, devices), jnp.float32),
            pltpu.VMEM((CAP - 1, devices, devices), jnp.float32),
        ],
        name="lists",
    )(me, read, shared)


def pick_kernel(list_ref, rows_ref, out_ref, wide_ref, stage_ref):
    group, room, _ = out_ref.shape
    step = pl.program_id(0)

    @pl.when(step == 0)
    def _():
        wide_ref[...] = rows_ref[...].astype(jnp.float32)

    for i in range(group):
        base = (step * group + i) * LIST
        stage = stage_ref.at[i % 2]
        for t in range(room):
            stage[pl.ds(t, 1), :] = wide_ref[pl.ds(list_ref[base + t], 1), :]
        out_ref[i] = stage[...].astype(out_ref.dtype)


def pick_rows(listed, rows, room):
    total, lanes = rows.shape
    devices, group = listed.shape[0] // LIST, 4
    return pl.pallas_call(
        pick_kernel,
        grid=(devices // group,),
        in_specs=[
            pl.BlockSpec(memory_space=pltpu.SMEM),
            pl.BlockSpec((total, lanes), lambda i: (0, 0), pipeline_mode=pl.Buffered(1)),
        ],
        out_specs=pl.BlockSpec((group, room, lanes), lambda i: (i, 0, 0)),
        out_shape=jax.ShapeDtypeStruct((devices, room, lanes), rows.dtype),
        scratch_shapes=[
            pltpu.VMEM((total, lanes), jnp.float32),
            pltpu.VMEM((2, room, lanes), jnp.float32),
        ],
        name="pick_rows",
    )(listed, rows)


def margin_kernel(plan_ref, own_ref, got_ref, out_ref, in_ref, wide_ref, block_ref, sum_ref, in_sem, out_sem):
    rows, room, lanes = got_ref.shape
    blocks = own_ref.shape[0]
    f32, bf16 = jnp.float32, jnp.bfloat16
    chunks = room // CHUNK
    copies = [
        pltpu.make_async_copy(
            got_ref.at[:, pl.ds(c * CHUNK, CHUNK), :], in_ref.at[c], in_sem.at[c]
        )
        for c in range(chunks)
    ]
    for copy in copies:
        copy.start()
    sum_ref[...] = jnp.zeros(sum_ref.shape, f32)
    block_ref[room] = jnp.zeros((rows, lanes), bf16)
    for b in range(blocks):
        block_ref[room + 1 + b] = own_ref[b]
    for c, copy in enumerate(copies):
        copy.wait()
        wide = wide_ref.at[c % 2]
        wide[...] = in_ref[c].astype(f32).reshape(rows * CHUNK, lanes)
        for t in range(CHUNK):
            block_ref[c * CHUNK + t] = wide[pl.ds(t, rows, stride=CHUNK), :].astype(bf16)

    def send(r):
        part = pl.ds(pl.multiple_of(r * rows, rows), rows)
        return pltpu.make_async_copy(sum_ref.at[part], out_ref.at[part], out_sem)

    def tiles(i):
        own = own_ref[plan_ref[CAP, i]]
        for j in range(CAP):
            spot = plan_ref[j, i]
            spot = jnp.where(spot < 0, room - 1 - spot, spot)
            yield lax.dot_general(
                own, block_ref[spot], (((1,), (1,)), ((), ())), preferred_element_type=f32
            ).astype(bf16).astype(f32)

    unroll = 2

    def step(q, carry):
        at = [q * unroll + u for u in range(unroll)]
        found = [list(tiles(i)) for i in at]
        for i, tile in zip(at, found):
            part = pl.ds(pl.multiple_of(plan_ref[CAP + 1, i] * rows, rows), rows)
            for j in range(CAP):
                sum_ref[part, j * rows : (j + 1) * rows] += tile[j]
        start = jnp.where(q == 0, 0, plan_ref[CAP + 1, at[0]])

        def leave(r, carry):
            send(r).start()
            return carry

        lax.fori_loop(start, plan_ref[CAP + 1, at[-1] + 1], leave, 0)
        return carry

    lax.fori_loop(0, blocks // unroll, step, 0)
    pltpu.make_async_copy(sum_ref, out_ref, out_sem).wait()


def margins(plan, own, got):
    rows, room, lanes = got.shape
    blocks = own.shape[0]
    return pl.pallas_call(
        margin_kernel,
        in_specs=[
            pl.BlockSpec(memory_space=pltpu.SMEM),
            pl.BlockSpec(memory_space=pltpu.VMEM),
            pl.BlockSpec(memory_space=pl.ANY),
        ],
        out_specs=pl.BlockSpec(memory_space=pl.ANY),
        out_shape=jax.ShapeDtypeStruct((RB_DEV * rows, CAP * rows), jnp.float32),
        scratch_shapes=[
            pltpu.VMEM((room // CHUNK, rows, CHUNK, lanes), got.dtype),
            pltpu.VMEM((2, rows * CHUNK, lanes), jnp.float32),
            pltpu.VMEM((room + 1 + blocks, rows, lanes), own.dtype),
            pltpu.VMEM((RB_DEV * rows, CAP * rows), jnp.float32),
            pltpu.SemaphoreType.DMA((room // CHUNK,)),
            pltpu.SemaphoreType.DMA,
        ],
        name="margins",
    )(plan, own, got)


def exchange(array):
    return lax.all_to_all(array, "dev", split_axis=0, concat_axis=0, tiled=True)


def shards(occurrence, block_owner, read_block, slot_order):
    devices = lax.axis_size("dev")
    blocks, _, kmers = occurrence.shape
    owner, read = block_owner.reshape(1, blocks), read_block.reshape(1, blocks)
    held_rows = exchange(occurrence.transpose(1, 0, 2))
    held_rows = held_rows.reshape(devices * blocks, kmers)
    own_row = jnp.concatenate(
        [slot_order, owner, jnp.zeros((1, devices - blocks), jnp.int32)], axis=1
    )
    shared = exchange(jnp.broadcast_to(own_row[:, None], (devices, 1, 2 * devices)))
    me = lax.axis_index("dev").astype(jnp.int32).reshape(1)
    listed, plan, branch = lists(me, read, shared.reshape(devices, 2 * devices))
    listed = listed.reshape(devices * LIST)

    def finish(room):
        outgoing = pick_rows(listed, held_rows, room)
        return margins(plan, occurrence, exchange(outgoing))

    rooms = ROOMS + ((CAP - 1) * blocks,)
    return lax.switch(branch[0], [lambda room=room: finish(room) for room in rooms])


def solution(mesh):
    placed = (P("dev", None, None), P("dev", None), P("dev"), P("dev", None))

    return jax.shard_map(
        shards, mesh=mesh, in_specs=placed, out_specs=P("dev", None), check_vma=False
    )
```

time: 345 us -> 156 us (0.45)
  blocking collectives: 194 us -> 58.9 us
  local copies, waits for them, and re-layouts: 54.1 us -> 6.58 us
  Pallas kernels: 0 us -> 45.1 us
  matrix products: 31.1 us -> 0 us
  waiting for transfers between devices: 51.7 us -> 27 us
  starting transfers between devices: 11.9 us -> 16.5 us
    all_to_all x1, blocking collectives: 194 us -> 58.9 us  [exchange(): return lax.all_to_all(array, 'dev', split_axis=0, concat_axis=0, tiled=True)]
    pallas_call x0 -> x3, Pallas kernels: none -> 45.1 us  [the longest x1 22.6 us: pick_rows(): pl.pallas_call(pick_kernel, grid=(devices // group,), in_specs=[pl.BlockS...]
    dot_general x3 -> x0, matrix products: 31.1 us -> none  [the longest x1 18.1 us: shards(): jnp.einsum('ns,sic->nic', placement, returned, preferred_element_type=jnp...]
    all_to_all x1 -> x2, waiting for transfers between devices: 51.7 us -> 27 us  [exchange(): return lax.all_to_all(array, 'dev', split_axis=0, concat_axis=0, tiled=True)]
    reshape x1 -> x0, local copies, waits for them, and re-layouts: 22.4 us -> none  [shards(): tile_block.astype(jnp.bfloat16).reshape(slot_total, rows, CAP * rows)]
    gather x2 -> x0, local copies, waits for them, and re-layouts: 19.3 us -> none  [the longest x1 14.1 us: shards(): tile_slot = tile_block[place_of]]
    dot_general x1 -> x0, local copies, waits for them, and re-layouts: 6.63 us -> none  [shards(): jnp.einsum('ns,sic->nic', placement, returned, preferred_element_type=jnp...]
    unnamed x8 -> x4, local copies, waits for them, and re-layouts: 0.02 us -> 5.07 us
  transfers between devices with their start and end apart: 1 -> 2, of which waited for: 1 -> 2; matrix products, arithmetic and copies ran while one was open for 0% -> 3% of each run, Pallas kernels for 0% -> 5%
where the time goes in v1:
time: 156 us
  blocking collectives  58.9 us (38%)
  Pallas kernels  45.1 us (29%)
  waiting for transfers between devices  27 us (17%)
  starting transfers between devices  16.5 us (11%)
  local copies, waits for them, and re-layouts  6.58 us (4%)
    all_to_all x1, blocking collectives, exchange(): return lax.all_to_all(array, 'dev', split_axis=0, concat_axis=0, tiled=True)  58.9 us
    all_to_all x2, waiting for transfers between devices, exchange(): return lax.all_to_all(array, 'dev', split_axis=0, concat_axis=0, tiled=True)  27 us
    pallas_call x1, Pallas kernels, pick_rows(): pl.pallas_call(pick_kernel, grid=(devices // group,), in_specs=[pl.BlockS...  22.6 us
    all_to_all x2, starting transfers between devices, exchange(): return lax.all_to_all(array, 'dev', split_axis=0, concat_axis=0, tiled=True)  16.5 us
    pallas_call x1, Pallas kernels, margins(): pl.pallas_call(margin_kernel, in_specs=[pl.BlockSpec(memory_space=pltpu.S...  15.3 us
    pallas_call x1, Pallas kernels, lists(): pl.pallas_call(lists_kernel, in_specs=[small, whole, whole], out_specs=(w...  7.24 us
    unnamed x4, local copies, waits for them, and re-layouts  5.07 us
  transfers between devices with their start and end apart: 2, of which 2 were waited for; matrix products, arithmetic and copies ran while one was open for 3% of the time, Pallas kernels for 5%

profile of v1, /device:TPU:1, one launch (start us, length us, event | category | flops | bytes accessed | tf_op | source)
XLA Modules:
  0.0 155.8 jit_solution(4594666889528955245)
XLA Ops:
  0.0 0.1 pad.2.clone
  0.1 0.7 add_add_fusion
  0.8 0.7 broadcast_in_dim.13
  1.5 11.5 %all-to-all-start.3 = ((s32[128,1,256]{2,1,0:T(1,128)}), s32[128,1,256]{2,1,0:T(1,128)S(1)}, u32[]{:S(2)}, u32[]{:S(2)}) async-start(s32[128,1,256]{2,1,0:T(1,128)} %broadcast_in_dim.13), calls=%async_computation.3 | async-start | bytes 262144 | tf_op jit(solution)/shard_map/all_to_all | solution.py:242
  13.0 0.0 copy-start
  13.0 4.4 %copy.16 = bf16[64,128,128]{2,0,1:T(8,128)(2,1)} copy(bf16[64,128,128]{2,1,0:T(8,128)(2,1)} %param.7) | data formatting | bytes 4194304 | tf_op args[0]
  17.4 5.6 %all-to-all-done.3 = s32[128,1,256]{2,1,0:T(1,128)S(1)} async-done(((s32[128,1,256]{2,1,0:T(1,128)}), s32[128,1,256]{2,1,0:T(1,128)S(1)}, u32[]{:S(2)}, u32[]{:S(2)}) %all-to-all-start.3) | async-done | bytes 131104 | tf_op jit(solution)/shard_map/all_to_all | solution.py:242
  23.0 5.0 %all-to-all-start.4 = ((bf16[128,64,128]{2,1,0:T(8,128)(2,1)}), bf16[128,64,128]{2,1,0:T(8,128)(2,1)}, u32[]{:S(2)}, u32[]{:S(2)}) async-start(bf16[128,64,128]{2,1,0:T(8,128)(2,1)} %bitcast.21), calls=%async_computation.4 | async-start | bytes 4194304 | tf_op jit(solution)/shard_map/all_to_all | solution.py:242
  28.0 0.7 copy.17
  28.6 7.2 %lists.1 = (s32[128,256]{1,0:T(8,128)S(1)}, s32[8,128]{1,0:T(8,128)S(1)}, s32[1]{0:T(128)}) custom-call(s32[1]{0:T(128)} %bitcast.3.me_ref, s32[1,64]{1,0:T(1,128)} %bitcast.31, s32[128,256]{1,0:T(8,128)} %bitcast.28), custom_call_target="tpu_custom_call" | custom-call | tf_op jit(solution)/shard_map/lists/pallas_call | solution.py:103
  36.4 21.4 %all-to-all-done.4 = bf16[128,64,128]{2,1,0:T(8,128)(2,1)} async-done(((bf16[128,64,128]{2,1,0:T(8,128)(2,1)}), bf16[128,64,128]{2,1,0:T(8,128)(2,1)}, u32[]{:S(2)}, u32[]{:S(2)}) %all-to-all-start.4) | async-done | bytes 2097184 | tf_op jit(solution)/shard_map/all_to_all | solution.py:242
  57.9 0.0 copy-done
  57.9 97.8 %conditional.1 = (f32[2048,512]{1,0:T(8,128)}) conditional(s32[]{:T(128)} %bitcast.7, (s32[128,256]{1,0:T(8,128)S(1)}, bf16[128,64,128]{2,1,0:T(8,128)(2,1)}, s32[8,128]{1,0:T(8,128)S(1)}, bf16[64,128,128]{2,1,0:T(8,128)(2,1)S(1)}) %tuple.21, (s32[128,256]{1,0:T(8,128)S(1)}, bf16[128,64,128]{2,1,0:T(8,128)(2,1)}, ...), branch_computations={%region_0.0_spmd, %region_1.0_spmd, %region_2.0_spmd} | conditional | bytes 12845064 | solution.py:264
  57.9 0.7 copy.11
  58.6 22.6 %pick_rows.3 = bf16[128,128,128]{2,1,0:T(8,128)(2,1)} custom-call(s32[32768]{0:T(1024)} %bitcast.26, bf16[8192,128]{1,0:T(8,128)(2,1)} %bitcast.rows_ref), custom_call_target="tpu_custom_call" | custom-call | tf_op jit(solution)/shard_map/cond/branch_0_fun/pick_rows/pallas_call | solution.py:141
  81.1 58.9 %all_to_all.22.got_ref = bf16[128,128,128]{2,1,0:T(8,128)(2,1)} all-to-all(bf16[128,128,128]{2,1,0:T(8,128)(2,1)} %pick_rows.3), channel_id=1, replica_groups=mesh['dev'=128] {'dev'}, dimensions={0} | all-to-all | bytes 8388608 | tf_op jit(solution)/shard_map/cond/branch_0_fun/all_to_all | solution.py:242
  140.1 15.3 %margins.3 = f32[2048,512]{1,0:T(8,128)} custom-call(s32[8,128]{1,0:T(8,128)S(1)} %get-tuple-element.32.plan_ref, bf16[64,128,128]{2,1,0:T(8,128)(2,1)S(1)} %get-tuple-element.34.own_ref, bf16[128,128,128]{2,1,0:T(8,128)(2,1)} %all_to_all.22.got_ref), custom_call_target="tpu_custom_call" | custom-call | tf_op jit(solution)/shard_map/cond/branch_0_fun/margins/pallas_call | solution.py:220
  (1 shorter events, 0.0 us)
Async XLA Ops:
  1.5 21.5 %all-to-all-start.3 = ((s32[128,1,256]{2,1,0:T(1,128)}), s32[128,1,256]{2,1,0:T(1,128)S(1)}, u32[]{:S(2)}, u32[]{:S(2)}) async-start(s32[128,1,256]{2,1,0:T(1,128)} %broadcast_in_dim.13), calls=%async_computation.3 | async-start | bytes 262144 | tf_op jit(solution)/shard_map/all_to_all | solution.py:242
  13.0 44.9 %copy-start = (bf16[64,128,128]{2,1,0:T(8,128)(2,1)S(1)}, bf16[64,128,128]{2,1,0:T(8,128)(2,1)}, u32[]{:S(2)}) copy-start(bf16[64,128,128]{2,1,0:T(8,128)(2,1)} %param.7) | copy-start | bytes 6291460
  23.0 34.9 %all-to-all-start.4 = ((bf16[128,64,128]{2,1,0:T(8,128)(2,1)}), bf16[128,64,128]{2,1,0:T(8,128)(2,1)}, u32[]{:S(2)}, u32[]{:S(2)}) async-start(bf16[128,64,128]{2,1,0:T(8,128)(2,1)} %bitcast.21), calls=%async_computation.4 | async-start | bytes 4194304 | tf_op jit(solution)/shard_map/all_to_all | solution.py:242

commit v2 on v1

--- a/solution.py
+++ b/solution.py
@@ -7,7 +7,6 @@
 
 CAP = 4
 RB_DEV = 16
-LIST = 256
 ROOMS = (128, 144)
 CHUNK = 16
 
@@ -62,9 +61,7 @@
         return found
 
     found = lax.fori_loop(0, devices, fill, jnp.zeros((most, devices), f32))
-    list_ref[:, :devices] = found[:devices].T.astype(jnp.int32)
-    rest = jnp.concatenate([found[devices:], jnp.zeros((LIST - most, devices), f32)], axis=0)
-    list_ref[:, devices:] = rest.T.astype(jnp.int32)
+    list_ref[:, 0, :] = found.astype(jnp.int32)
 
     me = me_ref[0].astype(f32)
 
@@ -105,7 +102,7 @@
         in_specs=[small, whole, whole],
         out_specs=(whole, whole, small),
         out_shape=(
-            jax.ShapeDtypeStruct((devices, LIST), jnp.int32),
+            jax.ShapeDtypeStruct(((CAP - 1) * read.shape[1], 1, devices), jnp.int32),
             jax.ShapeDtypeStruct((8, devices), jnp.int32),
             jax.ShapeDtypeStruct((1,), jnp.int32),
         ),
@@ -119,69 +116,94 @@
     )(me, read, shared)
 
 
-def pick_kernel(list_ref, rows_ref, out_ref, wide_ref, stage_ref):
+def pick_kernel(list_ref, rows_ref, out_ref, wide_ref, stage_ref, spare_ref, list_sem, *asked):
     group, room, _ = out_ref.shape
-    step = pl.program_id(0)
-
-    @pl.when(step == 0)
+    pairs = stage_ref.shape[0]
+
+    @pl.when(pl.program_id(0) == 0)
     def _():
+        copies = [
+            pltpu.make_async_copy(list_ref.at[t], asked[t], list_sem) for t in range(room)
+        ]
+        for copy in copies:
+            copy.start()
         wide_ref[...] = rows_ref[...].astype(jnp.float32)
-
-    for i in range(group):
-        base = (step * group + i) * LIST
-        stage = stage_ref.at[i % 2]
-        for t in range(room):
-            stage[pl.ds(t, 1), :] = wide_ref[pl.ds(list_ref[base + t], 1), :]
-        out_ref[i] = stage[...].astype(out_ref.dtype)
+        pltpu.make_async_copy(list_ref.at[pl.ds(0, room)], spare_ref, list_sem).wait()
+
+    first = pl.program_id(0) * group
+
+    def pick(i, carry):
+        for u in range(pairs):
+            at = i * pairs + u
+            s = first + at
+            for t in range(room):
+                stage_ref[u, pl.ds(t, 1), :] = wide_ref[pl.ds(asked[t][0, s], 1), :]
+            out_ref[at] = stage_ref[u].astype(out_ref.dtype)
+        return carry
+
+    lax.fori_loop(0, group // pairs, pick, 0)
 
 
 def pick_rows(listed, rows, room):
     total, lanes = rows.shape
-    devices, group = listed.shape[0] // LIST, 4
+    devices, group, pairs = listed.shape[2], 8, 2
     return pl.pallas_call(
         pick_kernel,
         grid=(devices // group,),
         in_specs=[
-            pl.BlockSpec(memory_space=pltpu.SMEM),
-            pl.BlockSpec((total, lanes), lambda i: (0, 0), pipeline_mode=pl.Buffered(1)),
+            pl.BlockSpec(memory_space=pltpu.VMEM),
+            pl.BlockSpec(memory_space=pltpu.VMEM),
         ],
         out_specs=pl.BlockSpec((group, room, lanes), lambda i: (i, 0, 0)),
         out_shape=jax.ShapeDtypeStruct((devices, room, lanes), rows.dtype),
         scratch_shapes=[
             pltpu.VMEM((total, lanes), jnp.float32),
-            pltpu.VMEM((2, room, lanes), jnp.float32),
-        ],
+            pltpu.VMEM((pairs, room, lanes), jnp.float32),
+            pltpu.SMEM((room, 1, devices), jnp.int32),
+            pltpu.SemaphoreType.DMA,
+        ]
+        + [pltpu.SMEM((1, devices), jnp.int32)] * room,
         name="pick_rows",
     )(listed, rows)
 
 
-def margin_kernel(plan_ref, own_ref, got_ref, out_ref, in_ref, wide_ref, block_ref, sum_ref, in_sem, out_sem):
+def margin_kernel(plan_ref, own_ref, got_ref, out_ref, in_ref, wide_ref, block_ref, sum_ref, other_ref, in_sem, out_sem):
     rows, room, lanes = got_ref.shape
     blocks = own_ref.shape[0]
     f32, bf16 = jnp.float32, jnp.bfloat16
     chunks = room // CHUNK
-    copies = [
-        pltpu.make_async_copy(
-            got_ref.at[:, pl.ds(c * CHUNK, CHUNK), :], in_ref.at[c], in_sem.at[c]
+    apart = CHUNK + 1
+
+    def fetch(c):
+        return pltpu.make_async_copy(
+            got_ref.at[:, pl.ds(pl.multiple_of(c * CHUNK, CHUNK), CHUNK), :], in_ref.at[c], in_sem.at[c]
         )
-        for c in range(chunks)
-    ]
-    for copy in copies:
-        copy.start()
+
+    for c in range(chunks):
+        fetch(c).start()
     sum_ref[...] = jnp.zeros(sum_ref.shape, f32)
+    other_ref[...] = jnp.zeros(other_ref.shape, f32)
     block_ref[room] = jnp.zeros((rows, lanes), bf16)
-    for b in range(blocks):
+
+    def keep(b, carry):
         block_ref[room + 1 + b] = own_ref[b]
-    for c, copy in enumerate(copies):
-        copy.wait()
-        wide = wide_ref.at[c % 2]
-        wide[...] = in_ref[c].astype(f32).reshape(rows * CHUNK, lanes)
+        return carry
+
+    lax.fori_loop(0, blocks, keep, 0, unroll=8)
+
+    def turn(c, carry):
+        fetch(c).wait()
+
+        def widen(d, carry):
+            wide_ref[pl.ds(d * apart, CHUNK), :] = in_ref[c, d].astype(f32)
+            return carry
+
+        lax.fori_loop(0, rows, widen, 0, unroll=16)
         for t in range(CHUNK):
-            block_ref[c * CHUNK + t] = wide[pl.ds(t, rows, stride=CHUNK), :].astype(bf16)
-
-    def send(r):
-        part = pl.ds(pl.multiple_of(r * rows, rows), rows)
-        return pltpu.make_async_copy(sum_ref.at[part], out_ref.at[part], out_sem)
+            block_ref[c * CHUNK + t] = wide_ref[pl.ds(t, rows, stride=apart), :].astype(bf16)
+        return carry
+
+    lax.fori_loop(0, chunks, turn, 0)
 
     def tiles(i):
         own = own_ref[plan_ref[CAP, i]]
@@ -192,25 +214,26 @@
                 own, block_ref[spot], (((1,), (1,)), ((), ())), preferred_element_type=f32
             ).astype(bf16).astype(f32)
 
-    unroll = 2
+    sums = (sum_ref, other_ref)
+    unroll = 4
 
     def step(q, carry):
-        at = [q * unroll + u for u in range(unroll)]
-        found = [list(tiles(i)) for i in at]
-        for i, tile in zip(at, found):
+        for u in range(unroll):
+            i = q * unroll + u
             part = pl.ds(pl.multiple_of(plan_ref[CAP + 1, i] * rows, rows), rows)
-            for j in range(CAP):
-                sum_ref[part, j * rows : (j + 1) * rows] += tile[j]
-        start = jnp.where(q == 0, 0, plan_ref[CAP + 1, at[0]])
-
-        def leave(r, carry):
-            send(r).start()
-            return carry
-
-        lax.fori_loop(start, plan_ref[CAP + 1, at[-1] + 1], leave, 0)
+            for j, tile in enumerate(tiles(i)):
+                sums[u % 2][part, j * rows : (j + 1) * rows] += tile
         return carry
 
     lax.fori_loop(0, blocks // unroll, step, 0)
+
+    def leave(r, carry):
+        part = pl.ds(pl.multiple_of(r * rows, rows), rows)
+        sum_ref[part] += other_ref[part]
+        pltpu.make_async_copy(sum_ref.at[part], out_ref.at[part], out_sem).start()
+        return carry
+
+    lax.fori_loop(0, RB_DEV, leave, 0)
     pltpu.make_async_copy(sum_ref, out_ref, out_sem).wait()
 
 
@@ -228,8 +251,9 @@
         out_shape=jax.ShapeDtypeStruct((RB_DEV * rows, CAP * rows), jnp.float32),
         scratch_shapes=[
             pltpu.VMEM((room // CHUNK, rows, CHUNK, lanes), got.dtype),
-            pltpu.VMEM((2, rows * CHUNK, lanes), jnp.float32),
+            pltpu.VMEM((rows * (CHUNK + 1), lanes), jnp.float32),
             pltpu.VMEM((room + 1 + blocks, rows, lanes), own.dtype),
+            pltpu.VMEM((RB_DEV * rows, CAP * rows), jnp.float32),
             pltpu.VMEM((RB_DEV * rows, CAP * rows), jnp.float32),
             pltpu.SemaphoreType.DMA((room // CHUNK,)),
             pltpu.SemaphoreType.DMA,
@@ -254,7 +278,6 @@
     shared = exchange(jnp.broadcast_to(own_row[:, None], (devices, 1, 2 * devices)))
     me = lax.axis_index("dev").astype(jnp.int32).reshape(1)
     listed, plan, branch = lists(me, read, shared.reshape(devices, 2 * devices))
-    listed = listed.reshape(devices * LIST)
 
     def finish(room):
         outgoing = pick_rows(listed, held_rows, room)

time: 156 us -> 145 us (0.929)
  Pallas kernels: 45.1 us -> 35.3 us
    pallas_call x1, Pallas kernels: 22.6 us -> 14.9 us  [pick_rows(): pl.pallas_call(pick_kernel, grid=(devices // group,), in_specs=[pl.BlockS...]
    pallas_call x1, Pallas kernels: 15.3 us -> 12.9 us  [margins(): pl.pallas_call(margin_kernel, in_specs=[pl.BlockSpec(memory_space=pltpu.S...]
  transfers between devices with their start and end apart: 2 -> 2, of which waited for: 2 -> 2; matrix products, arithmetic and copies ran while one was open for 3% -> 4% of each run, Pallas kernels for 5% -> 5%
where the time goes in v2:
time: 145 us
  blocking collectives  59 us (41%)
  Pallas kernels  35.3 us (24%)
  waiting for transfers between devices  26.8 us (18%)
  starting transfers between devices  16.5 us (11%)
  local copies, waits for them, and re-layouts  5.86 us (4%)
    all_to_all x1, blocking collectives, exchange(): return lax.all_to_all(array, 'dev', split_axis=0, concat_axis=0, tiled=True)  59 us
    all_to_all x2, waiting for transfers between devices, exchange(): return lax.all_to_all(array, 'dev', split_axis=0, concat_axis=0, tiled=True)  26.8 us
    all_to_all x2, starting transfers between devices, exchange(): return lax.all_to_all(array, 'dev', split_axis=0, concat_axis=0, tiled=True)  16.5 us
    pallas_call x1, Pallas kernels, pick_rows(): pl.pallas_call(pick_kernel, grid=(devices // group,), in_specs=[pl.BlockS...  14.9 us
    pallas_call x1, Pallas kernels, margins(): pl.pallas_call(margin_kernel, in_specs=[pl.BlockSpec(memory_space=pltpu.S...  12.9 us
    pallas_call x1, Pallas kernels, lists(): pl.pallas_call(lists_kernel, in_specs=[small, whole, whole], out_specs=(w...  7.46 us
    unnamed x4, local copies, waits for them, and re-layouts  5.07 us
  transfers between devices with their start and end apart: 2, of which 2 were waited for; matrix products, arithmetic and copies ran while one was open for 4% of the time, Pallas kernels for 5%

profile of v2, /device:TPU:1, one launch (start us, length us, event | category | flops | bytes accessed | tf_op | source)
XLA Modules:
  0.0 144.7 jit_solution(5588762423928889672)
XLA Ops:
  0.0 0.1 pad.2.clone
  0.1 0.7 add_add_fusion
  0.8 0.7 broadcast_in_dim.13
  1.5 11.5 %all-to-all-start.3 = ((s32[128,1,256]{2,1,0:T(1,128)}), s32[128,1,256]{2,1,0:T(1,128)S(1)}, u32[]{:S(2)}, u32[]{:S(2)}) async-start(s32[128,1,256]{2,1,0:T(1,128)} %broadcast_in_dim.13), calls=%async_computation.3 | async-start | bytes 262144 | tf_op jit(solution)/shard_map/all_to_all | solution.py:266
  13.0 0.0 copy-start
  13.0 4.4 %copy.13 = bf16[64,128,128]{2,0,1:T(8,128)(2,1)} copy(bf16[64,128,128]{2,1,0:T(8,128)(2,1)} %param.7) | data formatting | bytes 4194304 | tf_op args[0]
  17.4 5.6 %all-to-all-done.3 = s32[128,1,256]{2,1,0:T(1,128)S(1)} async-done(((s32[128,1,256]{2,1,0:T(1,128)}), s32[128,1,256]{2,1,0:T(1,128)S(1)}, u32[]{:S(2)}, u32[]{:S(2)}) %all-to-all-start.3) | async-done | bytes 131104 | tf_op jit(solution)/shard_map/all_to_all | solution.py:266
  23.0 5.0 %all-to-all-start.4 = ((bf16[128,64,128]{2,1,0:T(8,128)(2,1)}), bf16[128,64,128]{2,1,0:T(8,128)(2,1)}, u32[]{:S(2)}, u32[]{:S(2)}) async-start(bf16[128,64,128]{2,1,0:T(8,128)(2,1)} %bitcast.15), calls=%async_computation.4 | async-start | bytes 4194304 | tf_op jit(solution)/shard_map/all_to_all | solution.py:266
  28.0 0.7 copy.14
  28.6 7.5 %lists.1 = (s32[192,1,128]{2,1,0:T(1,128)S(1)}, s32[8,128]{1,0:T(8,128)S(1)}, s32[1]{0:T(128)}) custom-call(s32[1]{0:T(128)} %bitcast.3.me_ref, s32[1,64]{1,0:T(1,128)} %bitcast.19, s32[128,256]{1,0:T(8,128)} %bitcast.16), custom_call_target="tpu_custom_call" | custom-call | tf_op jit(solution)/shard_map/lists/pallas_call | solution.py:100
  36.6 21.2 %all-to-all-done.4 = bf16[128,64,128]{2,1,0:T(8,128)(2,1)} async-done(((bf16[128,64,128]{2,1,0:T(8,128)(2,1)}), bf16[128,64,128]{2,1,0:T(8,128)(2,1)}, u32[]{:S(2)}, u32[]{:S(2)}) %all-to-all-start.4) | async-done | bytes 2097184 | tf_op jit(solution)/shard_map/all_to_all | solution.py:266
  57.9 0.0 copy-done
  57.9 86.8 %conditional.1 = (f32[2048,512]{1,0:T(8,128)}) conditional(s32[]{:T(128)} %bitcast.7, (s32[192,1,128]{2,1,0:T(1,128)S(1)}, bf16[128,64,128]{2,1,0:T(8,128)(2,1)}, s32[8,128]{1,0:T(8,128)S(1)}, bf16[64,128,128]{2,1,0:T(8,128)(2,1)S(1)}) %tuple.21, (s32[192,1,128]{2,1,0:T(1,128)S(1)}, bf16[128,64,128]{2,1,0:T(8,128)(2,1)}, ...), branch_computations={%region_0.0_spmd, %region_1.0_spmd, %region_2.0_spmd} | conditional | bytes 12582920 | solution.py:287
  57.9 14.9 %pick_rows.3 = bf16[128,128,128]{2,1,0:T(8,128)(2,1)} custom-call(s32[192,1,128]{2,1,0:T(1,128)S(1)} %get-tuple-element.35.list_ref, bf16[8192,128]{1,0:T(8,128)(2,1)} %bitcast.rows_ref), custom_call_target="tpu_custom_call" | custom-call | tf_op jit(solution)/shard_map/cond/branch_0_fun/pick_rows/pallas_call | solution.py:150
  72.8 59.0 %all_to_all.22.got_ref = bf16[128,128,128]{2,1,0:T(8,128)(2,1)} all-to-all(bf16[128,128,128]{2,1,0:T(8,128)(2,1)} %pick_rows.3), channel_id=1, replica_groups=mesh['dev'=128] {'dev'}, dimensions={0} | all-to-all | bytes 8388608 | tf_op jit(solution)/shard_map/cond/branch_0_fun/all_to_all | solution.py:266
  131.8 12.9 %margins.3 = f32[2048,512]{1,0:T(8,128)} custom-call(s32[8,128]{1,0:T(8,128)S(1)} %get-tuple-element.32.plan_ref, bf16[64,128,128]{2,1,0:T(8,128)(2,1)S(1)} %get-tuple-element.34.own_ref, bf16[128,128,128]{2,1,0:T(8,128)(2,1)} %all_to_all.22.got_ref), custom_call_target="tpu_custom_call" | custom-call | tf_op jit(solution)/shard_map/cond/branch_0_fun/margins/pallas_call | solution.py:243
  (1 shorter events, 0.0 us)
Async XLA Ops:
  1.5 21.5 %all-to-all-start.3 = ((s32[128,1,256]{2,1,0:T(1,128)}), s32[128,1,256]{2,1,0:T(1,128)S(1)}, u32[]{:S(2)}, u32[]{:S(2)}) async-start(s32[128,1,256]{2,1,0:T(1,128)} %broadcast_in_dim.13), calls=%async_computation.3 | async-start | bytes 262144 | tf_op jit(solution)/shard_map/all_to_all | solution.py:266
  13.0 44.9 %copy-start = (bf16[64,128,128]{2,1,0:T(8,128)(2,1)S(1)}, bf16[64,128,128]{2,1,0:T(8,128)(2,1)}, u32[]{:S(2)}) copy-start(bf16[64,128,128]{2,1,0:T(8,128)(2,1)} %param.7) | copy-start | bytes 6291460
  23.0 34.9 %all-to-all-start.4 = ((bf16[128,64,128]{2,1,0:T(8,128)(2,1)}), bf16[128,64,128]{2,1,0:T(8,128)(2,1)}, u32[]{:S(2)}, u32[]{:S(2)}) async-start(bf16[128,64,128]{2,1,0:T(8,128)(2,1)} %bitcast.15), calls=%async_computation.4 | async-start | bytes 4194304 | tf_op jit(solution)/shard_map/all_to_all | solution.py:266

commit v3 on v2

--- a/solution.py
+++ b/solution.py
@@ -9,11 +9,69 @@
 RB_DEV = 16
 ROOMS = (128, 144)
 CHUNK = 16
-
-
-def lists_kernel(me_ref, read_ref, shared_ref, list_ref, plan_ref, most_ref, order_ref, owner_ref, rank_ref, value_ref):
+NOTES = 8
+
+
+def spread_kernel(order_ref, owner_ref, own_ref, out_ref, wide_ref, note_ref):
+    f32 = jnp.float32
+    blocks, rows, lanes = own_ref.shape
+    group = out_ref.shape[0]
+    apart = rows + 1
+    step = pl.program_id(0)
+
+    def iota(shape, axis):
+        return lax.broadcasted_iota(jnp.int32, shape, axis).astype(f32)
+
+    @pl.when(step == 0)
+    def _():
+        def widen(b, carry):
+            wide_ref[pl.ds(b * apart, rows), :] = own_ref[b].astype(f32)
+            return carry
+
+        lax.fori_loop(0, blocks, widen, 0, unroll=4)
+        row, lane = iota((rows, lanes), 0), iota((rows, lanes), 1)
+        order = order_ref[...].astype(f32)
+        by_row = jnp.sum(jnp.where(row == lane, order, 0.0), axis=1, keepdims=True)
+        place = jnp.sum(jnp.where(by_row == lane, row, 0.0), axis=0, keepdims=True)
+        column = iota((blocks, blocks), 1)
+        number = iota((blocks, blocks), 0)
+        owner = owner_ref[...].astype(f32)
+        owner = jnp.sum(jnp.where(number == column, owner, 0.0), axis=1, keepdims=True)
+        number = iota((blocks, lanes), 0)
+        held = jnp.where(owner == iota((blocks, lanes), 1), number + 1.0, 0.0)
+        held = jnp.sum(held, axis=0, keepdims=True)
+        rest = jnp.zeros((NOTES - 3, lanes), f32)
+        note_ref[...] = jnp.concatenate([order, place, held, rest], axis=0)
+
+    note = note_ref[...].astype(out_ref.dtype)
+    for i in range(group):
+        out_ref[i, :blocks] = wide_ref[pl.ds(step * group + i, blocks, stride=apart), :].astype(
+            out_ref.dtype
+        )
+        out_ref[i, blocks:] = note
+
+
+def spread(order, owner, own):
+    blocks, rows, lanes = own.shape
+    whole = pl.BlockSpec(memory_space=pltpu.VMEM)
+    group = 16
+    return pl.pallas_call(
+        spread_kernel,
+        grid=(rows // group,),
+        in_specs=[whole, whole, whole],
+        out_specs=pl.BlockSpec((group, blocks + NOTES, lanes), lambda i: (i, 0, 0)),
+        out_shape=jax.ShapeDtypeStruct((rows, blocks + NOTES, lanes), own.dtype),
+        scratch_shapes=[
+            pltpu.VMEM((blocks * (rows + 1), lanes), jnp.float32),
+            pltpu.VMEM((NOTES, lanes), jnp.float32),
+        ],
+        name="spread",
+    )(order, owner, own)
+
+
+def lists_kernel(me_ref, read_ref, note_ref, list_ref, plan_ref, most_ref, wide_ref, rank_ref, value_ref):
     f32, bf16 = jnp.float32, jnp.bfloat16
-    devices = shared_ref.shape[0]
+    devices = note_ref.shape[0]
     blocks = read_ref.shape[1]
     square = (devices, devices)
     most = (CAP - 1) * blocks
@@ -21,21 +79,16 @@
     def iota(shape, axis):
         return lax.broadcasted_iota(jnp.int32, shape, axis).astype(f32)
 
-    order = shared_ref[:, :devices]
-    order_ref[...] = order.astype(f32).T
-    owner_ref[...] = shared_ref[:, devices : 2 * devices].astype(f32).T
+    wide_ref[...] = note_ref[...].astype(f32).reshape(devices * NOTES, devices)
     row, lane = iota(square, 0), iota(square, 1)
 
-    def hold(n, held):
-        return jnp.where(owner_ref[pl.ds(n, 1), :] == row, (n + 1).astype(f32), held)
-
-    def stand(q, place):
-        return jnp.where(order_ref[pl.ds(q, 1), :] == row, q.astype(f32), place)
-
-    held = lax.fori_loop(0, blocks, hold, jnp.zeros(square, f32))
-    place = lax.fori_loop(0, devices, stand, jnp.zeros(square, f32)).T.astype(jnp.int32)
+    def noted(n):
+        return wide_ref[pl.ds(n, devices, stride=NOTES), :]
+
+    order, place = noted(0).astype(jnp.int32), noted(1).astype(jnp.int32)
+    held = noted(2).T
     there = jnp.take_along_axis(held, order, axis=1)
-    number = jnp.where(there > 0.0, order.astype(f32) * blocks + there, 0.0)
+    number = jnp.where(there > 0.0, order.astype(f32) * (blocks + NOTES) + there, 0.0)
     values = [
         jnp.where(held > 0.0, jnp.take_along_axis(number, place ^ j, axis=1), 0.0)
         for j in range(1, CAP)
@@ -93,31 +146,36 @@
     plan_ref[...] = jnp.concatenate(rows, axis=0).astype(jnp.int32)
 
 
-def lists(me, read, shared):
-    devices = shared.shape[0]
-    whole = pl.BlockSpec(memory_space=pltpu.VMEM)
+def lists(me, read, held_rows):
+    devices = held_rows.shape[0]
+    blocks = read.shape[1]
     small = pl.BlockSpec(memory_space=pltpu.SMEM)
+    square = pltpu.VMEM((CAP - 1, devices, devices), jnp.float32)
     return pl.pallas_call(
         lists_kernel,
-        in_specs=[small, whole, whole],
-        out_specs=(whole, whole, small),
+        grid=(1,),
+        in_specs=[
+            small,
+            pl.BlockSpec(memory_space=pltpu.VMEM),
+            pl.BlockSpec((devices, NOTES, devices), lambda i: (0, blocks // NOTES, 0)),
+        ],
+        out_specs=(
+            pl.BlockSpec(memory_space=pltpu.VMEM),
+            pl.BlockSpec(memory_space=pltpu.VMEM),
+            small,
+        ),
         out_shape=(
-            jax.ShapeDtypeStruct(((CAP - 1) * read.shape[1], 1, devices), jnp.int32),
+            jax.ShapeDtypeStruct(((CAP - 1) * blocks, 1, devices), jnp.int32),
             jax.ShapeDtypeStruct((8, devices), jnp.int32),
             jax.ShapeDtypeStruct((1,), jnp.int32),
         ),
-        scratch_shapes=[
-            pltpu.VMEM((devices, devices), jnp.float32),
-            pltpu.VMEM((devices, devices), jnp.float32),
-            pltpu.VMEM((CAP - 1, devices, devices), jnp.float32),
-            pltpu.VMEM((CAP - 1, devices, devices), jnp.float32),
-        ],
+        scratch_shapes=[pltpu.VMEM((devices * NOTES, devices), jnp.float32), square, square],
         name="lists",
-    )(me, read, shared)
+    )(me, read, held_rows)
 
 
 def pick_kernel(list_ref, rows_ref, out_ref, wide_ref, stage_ref, spare_ref, list_sem, *asked):
-    group, room, _ = out_ref.shape
+    group, room, lanes = out_ref.shape
     pairs = stage_ref.shape[0]
 
     @pl.when(pl.program_id(0) == 0)
@@ -215,7 +273,13 @@
             ).astype(bf16).astype(f32)
 
     sums = (sum_ref, other_ref)
-    unroll = 4
+    unroll = 8
+
+    def leave(r, carry):
+        part = pl.ds(pl.multiple_of(r * rows, rows), rows)
+        sum_ref[part] += other_ref[part]
+        pltpu.make_async_copy(sum_ref.at[part], out_ref.at[part], out_sem).start()
+        return carry
 
     def step(q, carry):
         for u in range(unroll):
@@ -223,17 +287,11 @@
             part = pl.ds(pl.multiple_of(plan_ref[CAP + 1, i] * rows, rows), rows)
             for j, tile in enumerate(tiles(i)):
                 sums[u % 2][part, j * rows : (j + 1) * rows] += tile
+        start = jnp.where(q == 0, 0, plan_ref[CAP + 1, q * unroll])
+        lax.fori_loop(start, plan_ref[CAP + 1, (q + 1) * unroll], leave, 0)
         return carry
 
     lax.fori_loop(0, blocks // unroll, step, 0)
-
-    def leave(r, carry):
-        part = pl.ds(pl.multiple_of(r * rows, rows), rows)
-        sum_ref[part] += other_ref[part]
-        pltpu.make_async_copy(sum_ref.at[part], out_ref.at[part], out_sem).start()
-        return carry
-
-    lax.fori_loop(0, RB_DEV, leave, 0)
     pltpu.make_async_copy(sum_ref, out_ref, out_sem).wait()
 
 
@@ -268,16 +326,12 @@
 
 def shards(occurrence, block_owner, read_block, slot_order):
     devices = lax.axis_size("dev")
-    blocks, _, kmers = occurrence.shape
+    blocks, rows, kmers = occurrence.shape
     owner, read = block_owner.reshape(1, blocks), read_block.reshape(1, blocks)
-    held_rows = exchange(occurrence.transpose(1, 0, 2))
-    held_rows = held_rows.reshape(devices * blocks, kmers)
-    own_row = jnp.concatenate(
-        [slot_order, owner, jnp.zeros((1, devices - blocks), jnp.int32)], axis=1
-    )
-    shared = exchange(jnp.broadcast_to(own_row[:, None], (devices, 1, 2 * devices)))
     me = lax.axis_index("dev").astype(jnp.int32).reshape(1)
-    listed, plan, branch = lists(me, read, shared.reshape(devices, 2 * devices))
+    held_rows = exchange(spread(slot_order, owner, occurrence))
+    listed, plan, branch = lists(me, read, held_rows)
+    held_rows = held_rows.reshape(devices * (blocks + NOTES), kmers)
 
     def finish(room):
         outgoing = pick_rows(listed, held_rows, room)
@@ -289,7 +343,6 @@
 
 def solution(mesh):
     placed = (P("dev", None, None), P("dev", None), P("dev"), P("dev", None))
-
     return jax.shard_map(
         shards, mesh=mesh, in_specs=placed, out_specs=P("dev", None), check_vma=False
     )

time: 145 us -> 139 us (0.959)
  waiting for transfers between devices: 26.8 us -> 32.9 us
  local copies, waits for them, and re-layouts: 5.86 us -> 0.01 us
  starting transfers between devices: 16.5 us -> 11.5 us
    all_to_all x2 -> x1, waiting for transfers between devices: 26.8 us -> 32.9 us  [exchange(): return lax.all_to_all(array, 'dev', split_axis=0, concat_axis=0, tiled=True)]
    unnamed x4 -> x0, local copies, waits for them, and re-layouts: 5.07 us -> none
    all_to_all x2 -> x1, starting transfers between devices: 16.5 us -> 11.5 us  [exchange(): return lax.all_to_all(array, 'dev', split_axis=0, concat_axis=0, tiled=True)]
    pallas_call x1 -> x2, Pallas kernels: 7.46 us -> 10.4 us  [the longest x1 5.24 us: lists(): pl.pallas_call(lists_kernel, grid=(1,), in_specs=[small, pl.BlockSpec(mem...]
    pallas_call x1, Pallas kernels: 12.9 us -> 11.1 us  [margins(): pl.pallas_call(margin_kernel, in_specs=[pl.BlockSpec(memory_space=pltpu.S...]
    pallas_call x1, Pallas kernels: 14.9 us -> 13.3 us  [pick_rows(): pl.pallas_call(pick_kernel, grid=(devices // group,), in_specs=[pl.BlockS...]
  transfers between devices with their start and end apart: 2 -> 1, of which waited for: 2 -> 1; matrix products, arithmetic and copies ran while one was open for 4% -> 0% of each run, Pallas kernels for 5% -> 0%
where the time goes in v3:
time: 139 us
  blocking collectives  59.1 us (43%)
  Pallas kernels  34.8 us (25%)
  waiting for transfers between devices  32.9 us (24%)
  starting transfers between devices  11.5 us (8%)
    all_to_all x1, blocking collectives, exchange(): return lax.all_to_all(array, 'dev', split_axis=0, concat_axis=0, tiled=True)  59.1 us
    all_to_all x1, waiting for transfers between devices, exchange(): return lax.all_to_all(array, 'dev', split_axis=0, concat_axis=0, tiled=True)  32.9 us
    pallas_call x1, Pallas kernels, pick_rows(): pl.pallas_call(pick_kernel, grid=(devices // group,), in_specs=[pl.BlockS...  13.3 us
    all_to_all x1, starting transfers between devices, exchange(): return lax.all_to_all(array, 'dev', split_axis=0, concat_axis=0, tiled=True)  11.5 us
    pallas_call x1, Pallas kernels, margins(): pl.pallas_call(margin_kernel, in_specs=[pl.BlockSpec(memory_space=pltpu.S...  11.1 us
    pallas_call x1, Pallas kernels, lists(): pl.pallas_call(lists_kernel, grid=(1,), in_specs=[small, pl.BlockSpec(mem...  5.24 us
    pallas_call x1, Pallas kernels, spread(): pl.pallas_call(spread_kernel, grid=(rows // group,), in_specs=[whole, who...  5.12 us
  transfers between devices with their start and end apart: 1, of which 1 were waited for; matrix products, arithmetic and copies ran while one was open for 0% of the time, Pallas kernels for 0%

profile of v3, /device:TPU:1, one launch (start us, length us, event | category | flops | bytes accessed | tf_op | source)
XLA Modules:
  0.0 139.0 jit_solution(18253230368492186239)
XLA Ops:
  0.0 5.1 %spread.1 = bf16[128,72,128]{2,1,0:T(8,128)(2,1)} custom-call(s32[1,128]{1,0:T(1,128)} %order_ref.1, s32[1,64]{1,0:T(1,128)} %bitcast.10, bf16[64,128,128]{2,1,0:T(8,128)(2,1)} %own_ref.1), custom_call_target="tpu_custom_call" | custom-call | tf_op jit(solution)/shard_map/spread/pallas_call | solution.py:58
  5.1 11.5 %all-to-all-start.3 = ((bf16[128,72,128]{2,1,0:T(8,128)(2,1)}), bf16[128,72,128]{2,1,0:T(8,128)(2,1)S(1)}, u32[]{:S(2)}, u32[]{:S(2)}) async-start(bf16[128,72,128]{2,1,0:T(8,128)(2,1)} %spread.1), calls=%async_computation.3 | async-start | bytes 4718592 | tf_op jit(solution)/shard_map/all_to_all | solution.py:324
  16.6 32.9 %all-to-all-done.3.note_ref = bf16[128,72,128]{2,1,0:T(8,128)(2,1)S(1)} async-done(((bf16[128,72,128]{2,1,0:T(8,128)(2,1)}), bf16[128,72,128]{2,1,0:T(8,128)(2,1)S(1)}, u32[]{:S(2)}, u32[]{:S(2)}) %all-to-all-start.3) | async-done | bytes 2359328 | tf_op jit(solution)/shard_map/all_to_all | solution.py:324
  49.5 5.2 %lists.1 = (s32[192,1,128]{2,1,0:T(1,128)S(1)}, s32[8,128]{1,0:T(8,128)S(1)}, s32[1]{0:T(128)}) custom-call(s32[1]{0:T(128)} %bitcast.3.me_ref, s32[1,64]{1,0:T(1,128)} %bitcast.11, bf16[128,72,128]{2,1,0:T(8,128)(2,1)S(1)} %all-to-all-done.3.note_ref), custom_call_target="tpu_custom_call" | custom-call | tf_op jit(solution)/shard_map/lists/pallas_call | solution.py:154
  55.4 83.5 %conditional.1 = (f32[2048,512]{1,0:T(8,128)}) conditional(s32[]{:T(128)} %bitcast.6, (s32[192,1,128]{2,1,0:T(1,128)S(1)}, bf16[128,72,128]{2,1,0:T(8,128)(2,1)S(1)}, s32[8,128]{1,0:T(8,128)S(1)}, bf16[64,128,128]{2,1,0:T(8,128)(2,1)}) %tuple.14, (s32[192,1,128]{2,1,0:T(1,128)S(1)}, bf16[128,72,128]{2,1,0:T(8,128)(2,1)S(1)}, ...), branch_computations={%region_0.0_spmd, %region_1.0_spmd, %region_2.0_spmd} | conditional | bytes 20971556 | solution.py:341
  55.4 13.3 %pick_rows.3 = bf16[128,128,128]{2,1,0:T(8,128)(2,1)} custom-call(s32[192,1,128]{2,1,0:T(1,128)S(1)} %get-tuple-element.35.list_ref, bf16[9216,128]{1,0:T(8,128)(2,1)S(1)} %bitcast.7), custom_call_target="tpu_custom_call" | custom-call | tf_op jit(solution)/shard_map/cond/branch_0_fun/pick_rows/pallas_call | solution.py:208
  68.8 0.0 copy-start
  68.8 59.1 %all_to_all.17.got_ref = bf16[128,128,128]{2,1,0:T(8,128)(2,1)} all-to-all(bf16[128,128,128]{2,1,0:T(8,128)(2,1)} %pick_rows.3), channel_id=1, replica_groups=mesh['dev'=128] {'dev'}, dimensions={0} | all-to-all | bytes 8388608 | tf_op jit(solution)/shard_map/cond/branch_0_fun/all_to_all | solution.py:324
  127.8 0.0 copy-done
  127.8 11.1 %margins.3 = f32[2048,512]{1,0:T(8,128)} custom-call(s32[8,128]{1,0:T(8,128)S(1)} %get-tuple-element.32.plan_ref, bf16[64,128,128]{2,1,0:T(8,128)(2,1)S(1)} %copy-done, bf16[128,128,128]{2,1,0:T(8,128)(2,1)} %all_to_all.17.got_ref), custom_call_target="tpu_custom_call" | custom-call | tf_op jit(solution)/shard_map/cond/branch_0_fun/margins/pallas_call | solution.py:301
Async XLA Ops:
  5.1 44.4 %all-to-all-start.3 = ((bf16[128,72,128]{2,1,0:T(8,128)(2,1)}), bf16[128,72,128]{2,1,0:T(8,128)(2,1)S(1)}, u32[]{:S(2)}, u32[]{:S(2)}) async-start(bf16[128,72,128]{2,1,0:T(8,128)(2,1)} %spread.1), calls=%async_computation.3 | async-start | bytes 4718592 | tf_op jit(solution)/shard_map/all_to_all | solution.py:324
  68.8 59.1 %copy-start = (bf16[64,128,128]{2,1,0:T(8,128)(2,1)S(1)}, bf16[64,128,128]{2,1,0:T(8,128)(2,1)}, u32[]{:S(2)}) copy-start(bf16[64,128,128]{2,1,0:T(8,128)(2,1)} %get-tuple-element.34.own_ref) | copy-start | bytes 6291460 | tf_op jit(solution)/shard_map/cond

commit v4 on v3

--- a/solution.py
+++ b/solution.py
@@ -12,7 +12,7 @@
 NOTES = 8
 
 
-def spread_kernel(order_ref, owner_ref, own_ref, out_ref, wide_ref, note_ref):
+def spread_kernel(order_ref, owner_ref, own_ref, out_ref, in_ref, wide_ref, note_ref, in_sem):
     f32 = jnp.float32
     blocks, rows, lanes = own_ref.shape
     group = out_ref.shape[0]
@@ -24,11 +24,21 @@
 
     @pl.when(step == 0)
     def _():
+        parts = [pl.ds(first, blocks // 4) for first in range(0, blocks, blocks // 4)]
+        copies = [
+            pltpu.make_async_copy(own_ref.at[part], in_ref.at[part], in_sem.at[c])
+            for c, part in enumerate(parts)
+        ]
+        for copy in copies:
+            copy.start()
+
         def widen(b, carry):
-            wide_ref[pl.ds(b * apart, rows), :] = own_ref[b].astype(f32)
+            wide_ref[pl.ds(b * apart, rows), :] = in_ref[b].astype(f32)
             return carry
 
-        lax.fori_loop(0, blocks, widen, 0, unroll=4)
+        for c, copy in enumerate(copies):
+            copy.wait()
+            lax.fori_loop(c * (blocks // 4), (c + 1) * (blocks // 4), widen, 0, unroll=4)
         row, lane = iota((rows, lanes), 0), iota((rows, lanes), 1)
         order = order_ref[...].astype(f32)
         by_row = jnp.sum(jnp.where(row == lane, order, 0.0), axis=1, keepdims=True)
@@ -54,27 +64,29 @@
 def spread(order, owner, own):
     blocks, rows, lanes = own.shape
     whole = pl.BlockSpec(memory_space=pltpu.VMEM)
-    group = 16
+    group = 32
     return pl.pallas_call(
         spread_kernel,
         grid=(rows // group,),
-        in_specs=[whole, whole, whole],
+        in_specs=[whole, whole, pl.BlockSpec(memory_space=pl.ANY)],
         out_specs=pl.BlockSpec((group, blocks + NOTES, lanes), lambda i: (i, 0, 0)),
         out_shape=jax.ShapeDtypeStruct((rows, blocks + NOTES, lanes), own.dtype),
         scratch_shapes=[
+            pltpu.VMEM(own.shape, own.dtype),
             pltpu.VMEM((blocks * (rows + 1), lanes), jnp.float32),
             pltpu.VMEM((NOTES, lanes), jnp.float32),
+            pltpu.SemaphoreType.DMA((4,)),
         ],
         name="spread",
     )(order, owner, own)
 
 
-def lists_kernel(me_ref, read_ref, note_ref, list_ref, plan_ref, most_ref, wide_ref, rank_ref, value_ref):
+def lists_kernel(note_ref, list_ref, most_ref, held_ref, place_ref, rank_ref, wide_ref, value_ref):
     f32, bf16 = jnp.float32, jnp.bfloat16
     devices = note_ref.shape[0]
-    blocks = read_ref.shape[1]
     square = (devices, devices)
-    most = (CAP - 1) * blocks
+    most = list_ref.shape[0]
+    blocks = most // (CAP - 1)
 
     def iota(shape, axis):
         return lax.broadcasted_iota(jnp.int32, shape, axis).astype(f32)
@@ -87,6 +99,8 @@
 
     order, place = noted(0).astype(jnp.int32), noted(1).astype(jnp.int32)
     held = noted(2).T
+    held_ref[...] = held
+    place_ref[...] = place
     there = jnp.take_along_axis(held, order, axis=1)
     number = jnp.where(there > 0.0, order.astype(f32) * (blocks + NOTES) + there, 0.0)
     values = [
@@ -97,25 +111,41 @@
     total = needs[0] + needs[1] + needs[2]
     below = (lane < row).astype(f32).astype(bf16)
     rank = jnp.dot(below, total.astype(bf16), preferred_element_type=f32)
-    ranks = []
     for j in range(CAP - 1):
-        ranks.append(jnp.where(needs[j] > 0.0, rank, -1.0))
+        rank_ref[j] = jnp.where(needs[j] > 0.0, rank, -1.0)
         rank = rank + needs[j]
-        rank_ref[j] = ranks[j]
         value_ref[j] = values[j] - 1.0
     count = jnp.max(rank[devices - 1 :, :])
     most_ref[0] = sum((count > room).astype(jnp.int32) for room in ROOMS)
-    turn = iota((most, devices), 0)
-
-    def fill(o, found):
-        for j in range(CAP - 1):
-            hit = rank_ref[j, pl.ds(o, 1), :] == turn
-            found = jnp.where(hit, value_ref[j, pl.ds(o, 1), :], found)
-        return found
-
-    found = lax.fori_loop(0, devices, fill, jnp.zeros((most, devices), f32))
-    list_ref[:, 0, :] = found.astype(jnp.int32)
-
+
+    def entries(first, length):
+        turn = iota((length, devices), 0) + float(first)
+
+        def fill(o, found):
+            for j in range(CAP - 1):
+                hit = rank_ref[j, pl.ds(o, 1), :] == turn
+                found = jnp.where(hit, value_ref[j, pl.ds(o, 1), :], found)
+            return found
+
+        found = lax.fori_loop(0, devices, fill, jnp.zeros((length, devices), f32), unroll=2)
+        list_ref[first : first + length, 0, :] = found.astype(jnp.int32)
+
+    entries(0, devices)
+
+    @pl.when(count > devices)
+    def _():
+        entries(devices, most - devices)
+
+
+def plan_kernel(me_ref, read_ref, held_ref, place_ref, rank_ref, plan_ref):
+    f32 = jnp.float32
+    devices = held_ref.shape[0]
+    blocks = read_ref.shape[1]
+
+    def iota(shape, axis):
+        return lax.broadcasted_iota(jnp.int32, shape, axis).astype(f32)
+
+    lane = iota((devices, devices), 1)
     me = me_ref[0].astype(f32)
 
     def mine(array):
@@ -126,13 +156,13 @@
     read = jnp.sum(jnp.where(row == column, reads, 0.0), axis=1, keepdims=True)
     before = (read < reads) | ((read == reads) & (row < column))
     at = jnp.sum(before.astype(f32), axis=0, keepdims=True)
-    own = mine(held)
+    own = mine(held_ref[...])
     chosen = own == iota((devices, blocks), 1) + 1.0
     at = jnp.sum(jnp.where(chosen, at, 0.0), axis=1, keepdims=True)
     read = jnp.sum(jnp.where(chosen, reads, 0.0), axis=1, keepdims=True)
     turn = (at == lane) & (own > 0.0)
-    stands = mine((place & (CAP - 1)).astype(f32))
-    spots = [-1.0 - own] + [mine(r) for r in ranks]
+    stands = mine((place_ref[...] & (CAP - 1)).astype(f32))
+    spots = [-1.0 - own] + [mine(rank_ref[j]) for j in range(CAP - 1)]
     rows = []
     for j in range(CAP):
         spot = jnp.zeros_like(own)
@@ -146,32 +176,40 @@
     plan_ref[...] = jnp.concatenate(rows, axis=0).astype(jnp.int32)
 
 
-def lists(me, read, held_rows):
+def lists(held_rows, blocks):
     devices = held_rows.shape[0]
-    blocks = read.shape[1]
+    whole = pl.BlockSpec(memory_space=pltpu.VMEM)
     small = pl.BlockSpec(memory_space=pltpu.SMEM)
-    square = pltpu.VMEM((CAP - 1, devices, devices), jnp.float32)
+    square = (devices, devices)
     return pl.pallas_call(
         lists_kernel,
         grid=(1,),
-        in_specs=[
-            small,
-            pl.BlockSpec(memory_space=pltpu.VMEM),
-            pl.BlockSpec((devices, NOTES, devices), lambda i: (0, blocks // NOTES, 0)),
-        ],
-        out_specs=(
-            pl.BlockSpec(memory_space=pltpu.VMEM),
-            pl.BlockSpec(memory_space=pltpu.VMEM),
-            small,
-        ),
+        in_specs=[pl.BlockSpec((devices, NOTES, devices), lambda i: (0, blocks // NOTES, 0))],
+        out_specs=(whole, small, whole, whole, whole),
         out_shape=(
             jax.ShapeDtypeStruct(((CAP - 1) * blocks, 1, devices), jnp.int32),
-            jax.ShapeDtypeStruct((8, devices), jnp.int32),
             jax.ShapeDtypeStruct((1,), jnp.int32),
+            jax.ShapeDtypeStruct(square, jnp.float32),
+            jax.ShapeDtypeStruct(square, jnp.int32),
+            jax.ShapeDtypeStruct((CAP - 1,) + square, jnp.float32),
         ),
-        scratch_shapes=[pltpu.VMEM((devices * NOTES, devices), jnp.float32), square, square],
+        scratch_shapes=[
+            pltpu.VMEM((devices * NOTES, devices), jnp.float32),
+            pltpu.VMEM((CAP - 1,) + square, jnp.float32),
+        ],
         name="lists",
-    )(me, read, held_rows)
+    )(held_rows)
+
+
+def planned(me, read, held, place, ranks):
+    whole = pl.BlockSpec(memory_space=pltpu.VMEM)
+    return pl.pallas_call(
+        plan_kernel,
+        in_specs=[pl.BlockSpec(memory_space=pltpu.SMEM)] + [whole] * 4,
+        out_specs=whole,
+        out_shape=jax.ShapeDtypeStruct((8, held.shape[0]), jnp.int32),
+        name="plan",
+    )(me, read, held, place, ranks)
 
 
 def pick_kernel(list_ref, rows_ref, out_ref, wide_ref, stage_ref, spare_ref, list_sem, *asked):
@@ -204,7 +242,7 @@
 
 def pick_rows(listed, rows, room):
     total, lanes = rows.shape
-    devices, group, pairs = listed.shape[2], 8, 2
+    devices, group, pairs = listed.shape[2], 16, 2
     return pl.pallas_call(
         pick_kernel,
         grid=(devices // group,),
@@ -330,11 +368,12 @@
     owner, read = block_owner.reshape(1, blocks), read_block.reshape(1, blocks)
     me = lax.axis_index("dev").astype(jnp.int32).reshape(1)
     held_rows = exchange(spread(slot_order, owner, occurrence))
-    listed, plan, branch = lists(me, read, held_rows)
+    listed, branch, held, place, ranks = lists(held_rows, blocks)
     held_rows = held_rows.reshape(devices * (blocks + NOTES), kmers)
 
     def finish(room):
         outgoing = pick_rows(listed, held_rows, room)
+        plan = planned(me, read, held, place, ranks)
         return margins(plan, occurrence, exchange(outgoing))
 
     rooms = ROOMS + ((CAP - 1) * blocks,)

time: 139 us -> 136 us (0.978)
  blocking collectives: 59.1 us -> 0 us
  waiting for transfers between devices: 32.9 us -> 84.9 us
  starting transfers between devices: 11.5 us -> 17.5 us
  Pallas kernels: 34.8 us -> 32.8 us
    all_to_all x1 -> x0, blocking collectives: 59.1 us -> none  [exchange(): return lax.all_to_all(array, 'dev', split_axis=0, concat_axis=0, tiled=True)]
    all_to_all x1 -> x2, waiting for transfers between devices: 32.9 us -> 84.9 us  [exchange(): return lax.all_to_all(array, 'dev', split_axis=0, concat_axis=0, tiled=True)]
    all_to_all x1 -> x2, starting transfers between devices: 11.5 us -> 17.5 us  [exchange(): return lax.all_to_all(array, 'dev', split_axis=0, concat_axis=0, tiled=True)]
    pallas_call x1 -> x2, Pallas kernels: 5.24 us -> 3.98 us  [the longest x1 3.14 us: lists(): pl.pallas_call(lists_kernel, grid=(1,), in_specs=[pl.BlockSpec((devices,...]
  transfers between devices with their start and end apart: 1 -> 2, of which waited for: 1 -> 2; matrix products, arithmetic and copies ran while one was open for 0% -> 0% of each run, Pallas kernels for 0% -> 1%
where the time goes in v4:
time: 136 us
  waiting for transfers between devices  84.9 us (62%)
  Pallas kernels  32.8 us (24%)
  starting transfers between devices  17.5 us (13%)
    all_to_all x2, waiting for transfers between devices, exchange(): return lax.all_to_all(array, 'dev', split_axis=0, concat_axis=0, tiled=True)  84.9 us
    all_to_all x2, starting transfers between devices, exchange(): return lax.all_to_all(array, 'dev', split_axis=0, concat_axis=0, tiled=True)  17.5 us
    pallas_call x1, Pallas kernels, pick_rows(): pl.pallas_call(pick_kernel, grid=(devices // group,), in_specs=[pl.BlockS...  13.3 us
    pallas_call x1, Pallas kernels, margins(): pl.pallas_call(margin_kernel, in_specs=[pl.BlockSpec(memory_space=pltpu.S...  11.2 us
    pallas_call x1, Pallas kernels, spread(): pl.pallas_call(spread_kernel, grid=(rows // group,), in_specs=[whole, who...  4.35 us
    pallas_call x1, Pallas kernels, lists(): pl.pallas_call(lists_kernel, grid=(1,), in_specs=[pl.BlockSpec((devices,...  3.14 us
  transfers between devices with their start and end apart: 2, of which 2 were waited for; matrix products, arithmetic and copies ran while one was open for 0% of the time, Pallas kernels for 1%

profile of v4, /device:TPU:1, one launch (start us, length us, event | category | flops | bytes accessed | tf_op | source)
XLA Modules:
  0.0 136.0 jit_solution(11747152885368049177)
XLA Ops:
  0.0 4.4 %spread.1 = bf16[128,72,128]{2,1,0:T(8,128)(2,1)} custom-call(s32[1,128]{1,0:T(1,128)} %order_ref.1, s32[1,64]{1,0:T(1,128)} %bitcast.17, bf16[64,128,128]{2,1,0:T(8,128)(2,1)} %own_ref.1), custom_call_target="tpu_custom_call" | custom-call | tf_op jit(solution)/shard_map/spread/pallas_call | solution.py:68
  4.4 0.0 copy-start.3
  4.4 11.5 %all-to-all-start.3 = ((bf16[128,72,128]{2,1,0:T(8,128)(2,1)}), bf16[128,72,128]{2,1,0:T(8,128)(2,1)S(1)}, u32[]{:S(2)}, u32[]{:S(2)}) async-start(bf16[128,72,128]{2,1,0:T(8,128)(2,1)} %spread.1), calls=%async_computation.3 | async-start | bytes 4718592 | tf_op jit(solution)/shard_map/all_to_all | solution.py:362
  15.9 32.9 %all-to-all-done.3.note_ref = bf16[128,72,128]{2,1,0:T(8,128)(2,1)S(1)} async-done(((bf16[128,72,128]{2,1,0:T(8,128)(2,1)}), bf16[128,72,128]{2,1,0:T(8,128)(2,1)S(1)}, u32[]{:S(2)}, u32[]{:S(2)}) %all-to-all-start.3) | async-done | bytes 2359328 | tf_op jit(solution)/shard_map/all_to_all | solution.py:362
  48.8 3.1 %lists.1 = (s32[192,1,128]{2,1,0:T(1,128)S(1)}, s32[1]{0:T(128)}, f32[128,128]{1,0:T(8,128)S(1)}, s32[128,128]{1,0:T(8,128)S(1)}, f32[3,128,128]{2,1,0:T(8,128)S(1)}) custom-call(bf16[128,72,128]{2,1,0:T(8,128)(2,1)S(1)} %all-to-all-done.3.note_ref), custom_call_target="tpu_custom_call" | custom-call | tf_op jit(solution)/shard_map/lists/pallas_call | solution.py:184
  52.6 0.0 copy-done.3
  52.6 83.4 %conditional.1 = (f32[2048,512]{1,0:T(8,128)}) conditional(s32[]{:T(128)} %bitcast.10, (s32[]{:T(128)}, s32[64]{0:T(128)S(1)}, f32[128,128]{1,0:T(8,128)S(1)}, s32[128,128]{1,0:T(8,128)S(1)}, f32[3,128,128]{2,1,0:T(8,128)S(1)}, /*index=5*/s32[192,1,128]{2,1,0:T(1,128)S(1)}, bf16[128,72,128]{2,1,0:T(8,128)(2,1)S(1)}, ...), branch_computations={%region_0.0_spmd, %region_1.0_spmd, %region_2.0_spmd} | conditional | bytes 27263044 | solution.py:380
  52.6 13.3 %pick_rows.3 = bf16[128,128,128]{2,1,0:T(8,128)(2,1)} custom-call(s32[192,1,128]{2,1,0:T(1,128)S(1)} %get-tuple-element.63.list_ref, bf16[9216,128]{1,0:T(8,128)(2,1)S(1)} %bitcast.11), custom_call_target="tpu_custom_call" | custom-call | tf_op jit(solution)/shard_map/cond/branch_0_fun/pick_rows/pallas_call | solution.py:246
  65.9 0.0 copy-start
  65.9 6.0 %all-to-all-start = ((bf16[128,128,128]{2,1,0:T(8,128)(2,1)}), bf16[128,128,128]{2,1,0:T(8,128)(2,1)}, u32[]{:S(2)}, u32[]{:S(2)}) async-start(bf16[128,128,128]{2,1,0:T(8,128)(2,1)} %pick_rows.3), calls=%async_computation | async-start | bytes 8388608 | tf_op jit(solution)/shard_map/cond/branch_0_fun/all_to_all | solution.py:362
  71.9 0.8 plan.3.plan_ref
  72.7 52.0 %all-to-all-done.got_ref = bf16[128,128,128]{2,1,0:T(8,128)(2,1)} async-done(((bf16[128,128,128]{2,1,0:T(8,128)(2,1)}), bf16[128,128,128]{2,1,0:T(8,128)(2,1)}, u32[]{:S(2)}, u32[]{:S(2)}) %all-to-all-start) | async-done | bytes 4194336 | tf_op jit(solution)/shard_map/cond/branch_0_fun/all_to_all | solution.py:362
  124.8 0.0 copy-done
  124.8 11.2 %margins.3 = f32[2048,512]{1,0:T(8,128)} custom-call(s32[8,128]{1,0:T(8,128)} %plan.3.plan_ref, bf16[64,128,128]{2,1,0:T(8,128)(2,1)S(1)} %copy-done, bf16[128,128,128]{2,1,0:T(8,128)(2,1)} %all-to-all-done.got_ref), custom_call_target="tpu_custom_call" | custom-call | tf_op jit(solution)/shard_map/cond/branch_0_fun/margins/pallas_call | solution.py:339
Async XLA Ops:
  4.4 48.2 %copy-start.3 = (s32[64]{0:T(128)S(1)}, s32[64]{0:T(128)}, u32[]{:S(2)}) copy-start(s32[64]{0:T(128)} %param.9) | copy-start | bytes 772
  4.4 44.4 %all-to-all-start.3 = ((bf16[128,72,128]{2,1,0:T(8,128)(2,1)}), bf16[128,72,128]{2,1,0:T(8,128)(2,1)S(1)}, u32[]{:S(2)}, u32[]{:S(2)}) async-start(bf16[128,72,128]{2,1,0:T(8,128)(2,1)} %spread.1), calls=%async_computation.3 | async-start | bytes 4718592 | tf_op jit(solution)/shard_map/all_to_all | solution.py:362
  65.9 58.9 %copy-start = (bf16[64,128,128]{2,1,0:T(8,128)(2,1)S(1)}, bf16[64,128,128]{2,1,0:T(8,128)(2,1)}, u32[]{:S(2)}) copy-start(bf16[64,128,128]{2,1,0:T(8,128)(2,1)} %get-tuple-element.62.own_ref) | copy-start | bytes 6291460 | tf_op jit(solution)/shard_map/cond
  65.9 58.9 %all-to-all-start = ((bf16[128,128,128]{2,1,0:T(8,128)(2,1)}), bf16[128,128,128]{2,1,0:T(8,128)(2,1)}, u32[]{:S(2)}, u32[]{:S(2)}) async-start(bf16[128,128,128]{2,1,0:T(8,128)(2,1)} %pick_rows.3), calls=%async_computation | async-start | bytes 8388608 | tf_op jit(solution)/shard_map/cond/branch_0_fun/all_to_all | solution.py:362
